TPU v7x, 32 devices: a whole 2x2x4 slice. The times are simulated.
32 devices in a mesh: stage: 4 (over z), expert: 8 (over y, x, core).
Axes of the slice: x: 2, y: 2, z: 4, core: 2. Of those that a mesh axis runs over, the one named last changes fastest.
Arguments:
- x_act: bfloat16 [4, 8192, 1024], P('stage', 'expert')
- route_idx: int32 [4, 8192, 2], P('stage', 'expert')
- route_gate: float32 [4, 8192, 2], P('stage', 'expert')
- w_up: bfloat16 [4, 16, 1024, 1024], P('stage', 'expert')
- w_lin: bfloat16 [4, 16, 1024, 1024], P('stage', 'expert')
- w_down: bfloat16 [4, 16, 1024, 1024], P('stage', 'expert')
- dy_out: bfloat16 [4, 8192, 1024], P('stage', 'expert')
Outputs:
- output 1: bfloat16 [4, 8192, 1024], P('stage', 'expert')
- output 2: bfloat16 [4, 8192, 1024], P('stage', 'expert')
- output 3: bfloat16 [4, 16, 1024, 1024], P('stage', 'expert')
- output 4: bfloat16 [4, 16, 1024, 1024], P('stage', 'expert')
- output 5: bfloat16 [4, 16, 1024, 1024], P('stage', 'expert')
All inputs are finite; a program needn't handle non-finite values.
Results may differ from a plain program's by a relative error of at most 0.001.
Values are sent between devices in bfloat16 or wider.
A program may use at most 1 GiB of HBM per device.

v0:
```python
import jax
import jax.numpy as jnp
from jax import lax
from jax.sharding import PartitionSpec as P


def slot_matrix(idx_tok, first_expert, num_local, capacity):
    tokens = idx_tok.shape[0]
    expert_ids = first_expert + jnp.arange(num_local, dtype=jnp.int32)
    is_expert = idx_tok[:, :, None] == expert_ids
    member = jnp.sum(is_expert, axis=1).astype(jnp.bfloat16)
    tok_ids = jnp.arange(tokens, dtype=jnp.int32)
    lower_tri = (tok_ids[:, None] > tok_ids[None, :]).astype(jnp.bfloat16)
    earlier = jnp.dot(lower_tri, member, preferred_element_type=jnp.float32).astype(jnp.int32)
    at_slot = earlier[:, :, None] == jnp.arange(capacity, dtype=jnp.int32)
    return (is_expert[:, :, :, None] & at_slot[:, None, :, :]).astype(jnp.bfloat16)


def expert_forward(x_rows, w_up, w_lin, w_down):
    pre_up = jnp.einsum("erd,edf->erf", x_rows, w_up, preferred_element_type=jnp.float32)
    pre_lin = jnp.einsum("erd,edf->erf", x_rows, w_lin, preferred_element_type=jnp.float32)
    act_up = jax.nn.silu(pre_up)
    hidden = (act_up * pre_lin).astype(jnp.bfloat16)
    out_rows = jnp.einsum("erf,efd->erd", hidden, w_down, preferred_element_type=jnp.float32).astype(jnp.bfloat16)
    return out_rows, (pre_up, pre_lin, act_up, hidden)


def expert_backward(x_rows, d_rows, w_up, w_lin, w_down, saved_acts):
    pre_up, pre_lin, act_up, hidden = saved_acts
    d_hidden = jnp.einsum("erd,efd->erf", d_rows, w_down, preferred_element_type=jnp.float32).astype(jnp.bfloat16).astype(jnp.float32)
    sigmoid_up = jax.nn.sigmoid(pre_up)
    d_up = (d_hidden * pre_lin * sigmoid_up * (1.0 + pre_up * (1.0 - sigmoid_up))).astype(jnp.bfloat16)
    d_lin = (d_hidden * act_up).astype(jnp.bfloat16)
    g_up = jnp.einsum("erd,erf->edf", x_rows, d_up, preferred_element_type=jnp.float32).astype(jnp.bfloat16)
    g_lin = jnp.einsum("erd,erf->edf", x_rows, d_lin, preferred_element_type=jnp.float32).astype(jnp.bfloat16)
    g_down = jnp.einsum("erf,erd->efd", hidden, d_rows, preferred_element_type=jnp.float32).astype(jnp.bfloat16)
    dx_rows = (jnp.einsum("erf,edf->erd", d_up, w_up, preferred_element_type=jnp.float32) + jnp.einsum("erf,edf->erd", d_lin, w_lin, preferred_element_type=jnp.float32)).astype(jnp.bfloat16)
    return dx_rows, g_up, g_lin, g_down


def solution(mesh):
    stages = mesh.shape["stage"]
    groups = mesh.shape["expert"]
    send_next = [(src, (src + 1) % stages) for src in range(stages)]
    send_back = [(src, (src - 1) % stages) for src in range(stages)]
    tok_spec = P("stage", "expert", None)
    w_spec = P("stage", "expert", None, None)

    def to_experts(slot_rows):
        num_experts, capacity, row_width = slot_rows.shape
        split_rows = slot_rows.reshape(groups, num_experts // groups, capacity, row_width)
        return lax.all_to_all(split_rows, "expert", 0, 2, tiled=True)[0]

    def to_owners(expert_rows):
        local_exp, gathered, row_width = expert_rows.shape
        back_rows = lax.all_to_all(expert_rows[None], "expert", 2, 0, tiled=True)
        return back_rows.reshape(groups * local_exp, gathered // groups, row_width)

    def device_step(x_act, route_idx, route_gate, w_up, w_lin, w_down, dy_out):
        tokens = x_act.shape[1]
        num_experts = w_up.shape[1] * groups
        capacity = 4 * tokens // num_experts
        x_tok = lax.ppermute(x_act[0], "stage", send_next)
        idx_tok = lax.ppermute(route_idx[0], "stage", send_next)
        gate_tok = lax.ppermute(route_gate[0], "stage", send_next)
        slot_place = slot_matrix(idx_tok, 0, num_experts, capacity)
        x_send = jnp.einsum("tjec,td->ecd", slot_place, x_tok, preferred_element_type=jnp.float32).astype(jnp.bfloat16)
        x_rows = to_experts(x_send)
        out_rows, saved_acts = expert_forward(x_rows, w_up[0], w_lin[0], w_down[0])
        out_copies = jnp.einsum("tjec,ecd->tjd", slot_place, to_owners(out_rows), preferred_element_type=jnp.float32)
        y_tok = jnp.sum(gate_tok[:, :, None] * out_copies, axis=1).astype(jnp.bfloat16)
        d_copies = (gate_tok[:, :, None] * dy_out[0][:, None, :].astype(jnp.float32)).astype(jnp.bfloat16)
        d_send = jnp.einsum("tjec,tjd->ecd", slot_place, d_copies, preferred_element_type=jnp.float32).astype(jnp.bfloat16)
        d_rows = to_experts(d_send)
        dx_rows, g_up, g_lin, g_down = expert_backward(x_rows, d_rows, w_up[0], w_lin[0], w_down[0], saved_acts)
        dx_tok = jnp.einsum("tjec,ecd->td", slot_place, to_owners(dx_rows), preferred_element_type=jnp.float32).astype(jnp.bfloat16)
        dx_prev = lax.ppermute(dx_tok, "stage", send_back)
        return y_tok[None], dx_prev[None], g_up[None], g_lin[None], g_down[None]

    return jax.shard_map(device_step, mesh=mesh, in_specs=(tok_spec, tok_spec, tok_spec, w_spec, w_spec, w_spec, tok_spec), out_specs=(tok_spec, tok_spec, w_spec, w_spec, w_spec), check_vma=False)
```

profile of v0, /device:TPU:0, one launch (start us, length us, event | category | flops | bytes accessed | tf_op | source)
XLA Modules:
  0.0 560.9 jit_solution(975140004146852362)
XLA Ops:
  10.7 20.0 %bitcast_convert_fusion = bf16[16,256,1024]{2,1,0:T(8,128)(2,1)} fusion(pred[1024,16,256]{0,2,1:T(8,128)(4,1)S(1)} %iota_compare_fusion, pred[1024,2,16]{0,1,2:T(4,128)(4,1)S(1)} %iota_compare_fusion.5, f32[1024,1024]{1,0:T(8,128)S(1)} %bitcast_convert_fusion.2, f32[1024,2]{0,1:T(2,128)S(1)} %collective-permute-done), kind=kOutput, calls=%fused_computation.12 | convolution fusion | flops 17196646400 | bytes 16818176 | tf_op jit(solution)/shard_map/tjec,tjd->ecd/dot_general | solution.py:73
  37.7 11.6 %convert_reduce_fusion = bf16[1024,16,256]{0,2,1:T(8,128)(2,1)} fusion(pred[1024,16,256]{0,2,1:T(8,128)(4,1)} %copy-done, pred[1024,2,16]{0,1,2:T(4,128)(4,1)S(1)} %iota_compare_fusion.5), kind=kLoop, calls=%fused_computation.5 | loop fusion | flops 29360128 | bytes 12615680 | tf_op jit(solution)/shard_map/tjec,td->ecd/reduce_sum | solution.py:67
  49.3 36.9 %collective-permute-done.2 = bf16[1024,1024]{1,0:T(8,128)(2,1)} collective-permute-done((bf16[1024,1024]{1,0:T(8,128)(2,1)S(1)}, bf16[1024,1024]{1,0:T(8,128)(2,1)}, u32[]{:S(2)}, u32[]{:S(2)}) %collective-permute-start.2) | collective-permute-done | bytes 2097184 | tf_op jit(solution)/shard_map/ppermute | solution.py:63
  86.2 14.8 %convolution_convert_fusion = bf16[16,256,1024]{2,1,0:T(8,128)(2,1)} fusion(bf16[1024,16,256]{0,2,1:T(8,128)(2,1)} %convert_reduce_fusion, bf16[1024,1024]{1,0:T(8,128)(2,1)} %collective-permute-done.2), kind=kOutput, calls=%fused_computation.27 | convolution fusion | flops 8589934592 | bytes 18874368 | tf_op jit(solution)/shard_map/tjec,td->ecd/dot_general | solution.py:67
  101.0 28.8 %all-to-all-done.2 = bf16[8,2,256,1024]{3,2,1,0:T(8,128)(2,1)} async-done(((bf16[8,2,256,1024]{3,2,1,0:T(8,128)(2,1)}), bf16[8,2,256,1024]{3,2,1,0:T(8,128)(2,1)}, u32[]{:S(2)}, u32[]{:S(2)}) %all-to-all-start.2) | async-done | bytes 8388640 | tf_op jit(solution)/shard_map/all_to_all | solution.py:52
  143.2 14.7 %convolution_convert_fusion.1 = bf16[2,2048,1024]{2,1,0:T(8,128)(2,1)} fusion(bf16[2,2048,1024]{2,1,0:T(8,128)(2,1)} %bitcast.94, bf16[1,2,1024,1024]{3,2,1,0:T(8,128)(2,1)S(1)} %copy-done.5), kind=kOutput, calls=%fused_computation.28 | convolution fusion | flops 8594128896 | bytes 20971520 | tf_op jit(solution)/shard_map/erd,efd->erf/dot_general | solution.py:30
  157.9 71.2 %all-to-all-done = bf16[8,2,256,1024]{3,2,1,0:T(8,128)(2,1)} async-done(((bf16[8,2,256,1024]{3,2,1,0:T(8,128)(2,1)}), bf16[8,2,256,1024]{3,2,1,0:T(8,128)(2,1)}, u32[]{:S(2)}, u32[]{:S(2)}) %all-to-all-start) | async-done | bytes 8388640 | tf_op jit(solution)/shard_map/all_to_all | solution.py:52
  229.1 8.1 %copy.21 = bf16[1,2,8,256,1024]{4,3,2,1,0:T(8,128)(2,1)} copy(bf16[1,2,8,256,1024]{4,3,1,2,0:T(8,128)(2,1)} %bitcast.6) | data formatting | bytes 16777216 | tf_op jit(solution)/shard_map/all_to_all | solution.py:52
  237.2 14.6 %fusion.26 = f32[2,2048,1024]{2,1,0:T(8,128)} fusion(bf16[2,2048,1024]{2,1,0:T(8,128)(2,1)} %bitcast.90, bf16[1,2,1024,1024]{3,2,1,0:T(8,128)(2,1)S(1)} %copy-done.4), kind=kOutput, calls=%fused_computation.38 | convolution fusion | flops 8589934592 | bytes 29360128 | tf_op jit(solution)/shard_map/erd,edf->erf/dot_general | solution.py:20
  251.8 28.9 %fusion.6 = (bf16[2,2048,1024]{2,1,0:T(8,128)(2,1)}, bf16[2,2048,1024]{2,1,0:T(8,128)(2,1)}, bf16[2,2048,1024]{2,1,0:T(8,128)(2,1)}) fusion(bf16[2,2048,1024]{2,1,0:T(8,128)(2,1)} %convolution_convert_fusion.1, f32[2,2048,1024]{2,1,0:T(8,128)} %fusion.26, bf16[2,2048,1024]{2,1,0:T(8,128)(2,1)} %bitcast.91, bf16[1,2,1024,1024]{3,2,1,0:T(8,128)(2,1)} %param.11), kind=kOutput, calls=%fused_computation.10 | convolution fusion | flops 8657043456 | bytes 62914560 | tf_op jit(solution)/shard_map/erd,edf->erf/dot_general | solution.py:21
  280.7 14.6 %fusion.24 = f32[2,2048,1024]{2,1,0:T(8,128)} fusion(bf16[2,2048,1024]{2,1,0:T(8,128)(2,1)} %get-tuple-element.5, bf16[1,2,1024,1024]{3,2,1,0:T(8,128)(2,1)S(1)} %copy-done.4), kind=kOutput, calls=%fused_computation.36 | convolution fusion | flops 8589934592 | bytes 29360128 | tf_op jit(solution)/shard_map/erf,edf->erd/dot_general | solution.py:37
  295.3 16.9 %fusion.13 = bf16[1,2,2048,1024]{3,2,1,0:T(8,128)(2,1)} fusion(f32[2,2048,1024]{2,1,0:T(8,128)} %fusion.24, bf16[2,2048,1024]{2,1,0:T(8,128)(2,1)} %get-tuple-element.7, bf16[1,2,1024,1024]{3,2,1,0:T(8,128)(2,1)} %param.11), kind=kOutput, calls=%fused_computation.22 | convolution fusion | flops 8598323200 | bytes 37748736 | tf_op jit(solution)/shard_map/erf,edf->erd/dot_general | solution.py:37
  312.2 16.4 %copy.26 = bf16[1,2,2048,1024]{3,1,0,2:T(2,128)(2,1)} copy(bf16[1,2,2048,1024]{3,2,1,0:T(8,128)(2,1)} %fusion.13) | data formatting | bytes 16777216 | tf_op jit(solution)/shard_map/broadcast_in_dim | solution.py:56
  333.8 12.5 %convert_bitcast_fusion = bf16[1,2,2048,1024]{3,2,1,0:T(8,128)(2,1)S(1)} fusion(bf16[2,2048,1024]{2,1,0:T(8,128)(2,1)} %get-tuple-element.6, bf16[1,2,1024,1024]{3,2,1,0:T(8,128)(2,1)} %param.12), kind=kOutput, calls=%fused_computation.26 | convolution fusion | flops 8594128896 | bytes 20971520 | tf_op jit(solution)/shard_map/erf,efd->erd/dot_general | solution.py:24
  346.3 29.2 %copy.22 = bf16[1,2,2048,1024]{3,1,0,2:T(2,128)(2,1)} copy(bf16[1,2,2048,1024]{3,2,1,0:T(8,128)(2,1)S(1)} %convert_bitcast_fusion) | data formatting | bytes 16777216 | tf_op jit(solution)/shard_map/broadcast_in_dim | solution.py:56
  375.5 15.0 %convert_bitcast_fusion.1 = bf16[1,2,1024,1024]{3,2,1,0:T(8,128)(2,1)} fusion(bf16[2,2048,1024]{2,1,0:T(8,128)(2,1)} %get-tuple-element.6, bf16[2,2048,1024]{2,1,0:T(8,128)(2,1)} %bitcast.95), kind=kOutput, calls=%fused_computation.40 | convolution fusion | flops 8592031744 | bytes 20971520 | tf_op jit(solution)/shard_map/erf,erd->efd/dot_general | solution.py:36
  390.6 37.2 %all-to-all-done.3 = bf16[1,2,2048,1024]{3,1,0,2:T(2,128)(2,1)} async-done(((bf16[1,2,2048,1024]{3,1,0,2:T(2,128)(2,1)}), bf16[1,2,2048,1024]{3,1,0,2:T(2,128)(2,1)}, u32[]{:S(2)}, u32[]{:S(2)}) %all-to-all-start.3) | async-done | bytes 8388640 | tf_op jit(solution)/shard_map/all_to_all | solution.py:56
  433.0 15.1 %convert_bitcast_fusion.3 = bf16[1,2,1024,1024]{3,2,1,0:T(8,128)(2,1)} fusion(bf16[2,2048,1024]{2,1,0:T(8,128)(2,1)} %bitcast.92, bf16[2,2048,1024]{2,1,0:T(8,128)(2,1)} %get-tuple-element.5), kind=kOutput, calls=%fused_computation.42 | convolution fusion | flops 8592031744 | bytes 20971520 | tf_op jit(solution)/shard_map/erd,erf->edf/dot_general | solution.py:34
  448.1 15.0 %convert_bitcast_fusion.2 = bf16[1,2,1024,1024]{3,2,1,0:T(8,128)(2,1)} fusion(bf16[2,2048,1024]{2,1,0:T(8,128)(2,1)} %bitcast.93, bf16[2,2048,1024]{2,1,0:T(8,128)(2,1)} %get-tuple-element.7), kind=kOutput, calls=%fused_computation.41 | convolution fusion | flops 8592031744 | bytes 20971520 | tf_op jit(solution)/shard_map/erd,erf->edf/dot_general | solution.py:35
  463.1 9.3 %copy.27 = bf16[1,2,8,256,1024]{4,3,1,2,0:T(8,128)(2,1)} copy(bf16[1,2,8,256,1024]{4,1,3,2,0:T(2,128)(2,1)} %bitcast.28) | data formatting | bytes 16777216 | tf_op jit(solution)/shard_map/all_to_all | solution.py:56
  472.5 14.9 %bitcast_convert_fusion.1 = bf16[1024,1024]{1,0:T(8,128)(2,1)} fusion(bf16[1024,16,256]{0,2,1:T(8,128)(2,1)} %convert_reduce_fusion, bf16[16,256,1024]{2,1,0:T(8,128)(2,1)} %bitcast.99), kind=kOutput, calls=%fused_computation.30 | convolution fusion | flops 8589934592 | bytes 18874368 | tf_op jit(solution)/shard_map/tjec,ecd->td/dot_general | solution.py:76
  489.6 37.4 %all-to-all-done.1 = bf16[1,2,2048,1024]{3,1,0,2:T(2,128)(2,1)} async-done(((bf16[1,2,2048,1024]{3,1,0,2:T(2,128)(2,1)}), bf16[1,2,2048,1024]{3,1,0,2:T(2,128)(2,1)}, u32[]{:S(2)}, u32[]{:S(2)}) %all-to-all-start.1) | async-done | bytes 8388640 | tf_op jit(solution)/shard_map/all_to_all | solution.py:56
  527.0 9.5 %copy.23 = bf16[1,2,8,256,1024]{4,3,1,2,0:T(8,128)(2,1)} copy(bf16[1,2,8,256,1024]{4,1,3,2,0:T(2,128)(2,1)} %bitcast.12) | data formatting | bytes 16777216 | tf_op jit(solution)/shard_map/all_to_all | solution.py:56
  536.5 22.6 %fusion.14 = bf16[1024,1024]{1,0:T(8,128)(2,1)} fusion(f32[1024,2]{0,1:T(2,128)S(1)} %copy-done.8, bf16[16,256,1024,1]{2,1,3,0:T(8,128)(2,1)} %bitcast.98, pred[1024,16,256]{0,2,1:T(8,128)(4,1)S(1)} %copy-done.1, pred[1024,2,16]{0,1,2:T(4,128)(4,1)S(1)} %copy-done.3), kind=kOutput, calls=%fused_computation.24 | convolution fusion | flops 17191403520 | bytes 14721024 | tf_op jit(solution)/shard_map/tjec,ecd->tjd/dot_general | solution.py:70
  (36 shorter events, 44.2 us)
Async XLA Ops:
  0.6 6.8 %collective-permute-start.1 = (s32[1024,2]{0,1:T(2,128)}, s32[1024,2]{0,1:T(2,128)S(1)}, u32[]{:S(2)}, u32[]{:S(2)}) collective-permute-start(s32[1024,2]{0,1:T(2,128)} %bitcast.102), channel_id=1, source_target_pairs={{0,8},{8,16},{16,24},{24,0},{1,9},{9,17},{17,25},{25,1},{2,10},{10... | collective-permute-start | bytes 24584 | tf_op jit(solution)/shard_map/ppermute | solution.py:64
  3.8 6.9 %collective-permute-start = (f32[1024,2]{0,1:T(2,128)}, f32[1024,2]{0,1:T(2,128)S(1)}, u32[]{:S(2)}, u32[]{:S(2)}) collective-permute-start(f32[1024,2]{0,1:T(2,128)} %bitcast.103), channel_id=1, source_target_pairs={{0,8},{8,16},{16,24},{24,0},{1,9},{9,17},{17,25},{25,1},{2,10},{10... | collective-permute-start | bytes 24584 | tf_op jit(solution)/shard_map/ppermute | solution.py:65
  10.5 20.1 %copy-start = (pred[1024,16,256]{0,2,1:T(8,128)(4,1)}, pred[1024,16,256]{0,2,1:T(8,128)(4,1)S(1)}, u32[]{:S(2)}) copy-start(pred[1024,16,256]{0,2,1:T(8,128)(4,1)S(1)} %iota_compare_fusion) | copy-start | bytes 12582916
  10.6 27.0 %copy-start.2 = (pred[1024,2,16]{0,1,2:T(4,128)(4,1)}, pred[1024,2,16]{0,1,2:T(4,128)(4,1)S(1)}, u32[]{:S(2)}) copy-start(pred[1024,2,16]{0,1,2:T(4,128)(4,1)S(1)} %iota_compare_fusion.5) | copy-start | bytes 98308
  10.7 20.0 %copy-start.7 = (f32[1024,2]{0,1:T(2,128)}, f32[1024,2]{0,1:T(2,128)S(1)}, u32[]{:S(2)}) copy-start(f32[1024,2]{0,1:T(2,128)S(1)} %collective-permute-done) | copy-start | bytes 24580
  30.7 5.2 copy-start.6
  30.7 99.2 %all-to-all-start.2 = ((bf16[8,2,256,1024]{3,2,1,0:T(8,128)(2,1)}), bf16[8,2,256,1024]{3,2,1,0:T(8,128)(2,1)}, u32[]{:S(2)}, u32[]{:S(2)}) async-start(bf16[8,2,256,1024]{3,2,1,0:T(8,128)(2,1)} %bitcast.96), calls=%async_computation.2 | async-start | bytes 16777216 | tf_op jit(solution)/shard_map/all_to_all | solution.py:52
  35.9 50.3 %collective-permute-start.2 = (bf16[1024,1024]{1,0:T(8,128)(2,1)S(1)}, bf16[1024,1024]{1,0:T(8,128)(2,1)}, u32[]{:S(2)}, u32[]{:S(2)}) collective-permute-start(bf16[1024,1024]{1,0:T(8,128)(2,1)S(1)} %bitcast.101), channel_id=1, source_target_pairs={{0,8},{8,16},{16,24},{24,0},{1,9},{9,17},{17,25},{25,1},{2,10},{10... | collective-permute-start | bytes 6291464 | tf_op jit(solution)/shard_map/ppermute | solution.py:63
  129.9 99.3 %all-to-all-start = ((bf16[8,2,256,1024]{3,2,1,0:T(8,128)(2,1)}), bf16[8,2,256,1024]{3,2,1,0:T(8,128)(2,1)}, u32[]{:S(2)}, u32[]{:S(2)}) async-start(bf16[8,2,256,1024]{3,2,1,0:T(8,128)(2,1)} %bitcast.97), calls=%async_computation | async-start | bytes 16777216 | tf_op jit(solution)/shard_map/all_to_all | solution.py:52
  135.1 8.1 %copy-start.5 = (bf16[1,2,1024,1024]{3,2,1,0:T(8,128)(2,1)S(1)}, bf16[1,2,1024,1024]{3,2,1,0:T(8,128)(2,1)}, u32[]{:S(2)}) copy-start(bf16[1,2,1024,1024]{3,2,1,0:T(8,128)(2,1)} %param.12) | copy-start | bytes 12582916
  229.1 8.1 %copy-start.4 = (bf16[1,2,1024,1024]{3,2,1,0:T(8,128)(2,1)S(1)}, bf16[1,2,1024,1024]{3,2,1,0:T(8,128)(2,1)}, u32[]{:S(2)}) copy-start(bf16[1,2,1024,1024]{3,2,1,0:T(8,128)(2,1)} %param.10) | copy-start | bytes 12582916
  328.6 99.1 %all-to-all-start.3 = ((bf16[1,2,2048,1024]{3,1,0,2:T(2,128)(2,1)}), bf16[1,2,2048,1024]{3,1,0,2:T(2,128)(2,1)}, u32[]{:S(2)}, u32[]{:S(2)}) async-start(bf16[1,2,2048,1024]{3,1,0,2:T(2,128)(2,1)} %copy.26), calls=%async_computation.3 | async-start | bytes 16777216 | tf_op jit(solution)/shard_map/all_to_all | solution.py:56
  427.8 99.3 %all-to-all-start.1 = ((bf16[1,2,2048,1024]{3,1,0,2:T(2,128)(2,1)}), bf16[1,2,2048,1024]{3,1,0,2:T(2,128)(2,1)}, u32[]{:S(2)}, u32[]{:S(2)}) async-start(bf16[1,2,2048,1024]{3,1,0,2:T(2,128)(2,1)} %copy.22), calls=%async_computation.1 | async-start | bytes 16777216 | tf_op jit(solution)/shard_map/all_to_all | solution.py:56
  487.4 71.7 %collective-permute-start.3 = (bf16[1024,1024]{1,0:T(8,128)(2,1)}, bf16[1024,1024]{1,0:T(8,128)(2,1)S(1)}, u32[]{:S(2)}, u32[]{:S(2)}) collective-permute-start(bf16[1024,1024]{1,0:T(8,128)(2,1)} %bitcast_convert_fusion.1), channel_id=1, source_target_pairs={{0,24},{8,0},{16,8},{24,16},{1,25},{9,1},{17,9},{25,17},{2,26},{10... | collective-permute-start | bytes 6291464 | tf_op jit(solution)/shard_map/ppermute | solution.py:77
  527.0 9.5 %copy-start.1 = (pred[1024,16,256]{0,2,1:T(8,128)(4,1)S(1)}, pred[1024,16,256]{0,2,1:T(8,128)(4,1)}, u32[]{:S(2)}) copy-start(pred[1024,16,256]{0,2,1:T(8,128)(4,1)} %copy-done) | copy-start | bytes 12582916
  527.0 9.5 %copy-start.3 = (pred[1024,2,16]{0,1,2:T(4,128)(4,1)S(1)}, pred[1024,2,16]{0,1,2:T(4,128)(4,1)}, u32[]{:S(2)}) copy-start(pred[1024,2,16]{0,1,2:T(4,128)(4,1)} %copy-done.2) | copy-start | bytes 98308
  527.0 9.5 %copy-start.8 = (f32[1024,2]{0,1:T(2,128)S(1)}, f32[1024,2]{0,1:T(2,128)}, u32[]{:S(2)}) copy-start(f32[1024,2]{0,1:T(2,128)} %copy-done.7) | copy-start | bytes 24580
where the time goes:
time: 567 us; the launch traced here: 561 us
  matrix products  220 us (39%)
  waiting for transfers between devices  211 us (37%)
  local copies, waits for them, and re-layouts  82 us (14%)
  starting transfers between devices  29.6 us (5%)
  other arithmetic  16.4 us (3%)
    all_to_all x2, waiting for transfers between devices, to_experts(): return lax.all_to_all(split_rows, 'expert', 0, 2, tiled=True)[0]  100 us
    all_to_all x2, waiting for transfers between devices, to_owners(): back_rows = lax.all_to_all(expert_rows[None], 'expert', 2, 0, tiled=True)  74.6 us
    broadcast_in_dim x2, local copies, waits for them, and re-layouts, to_owners(): back_rows = lax.all_to_all(expert_rows[None], 'expert', 2, 0, tiled=True)  45.6 us
    ppermute x1, waiting for transfers between devices, device_step(): x_tok = lax.ppermute(x_act[0], 'stage', send_next)  36.9 us
    dot_general x1, matrix products, expert_forward(): jnp.einsum('erd,edf->erf', x_rows, w_lin, preferred_element_type=jnp.floa...  28.9 us
    dot_general x1, matrix products, device_step(): jnp.einsum('tjec,ecd->tjd', slot_place, to_owners(out_rows), preferred_el...  22.6 us
    dot_general x1, matrix products, device_step(): jnp.einsum('tjec,tjd->ecd', slot_place, d_copies, preferred_element_type=...  20 us
    all_to_all x2, local copies, waits for them, and re-layouts, to_owners(): back_rows = lax.all_to_all(expert_rows[None], 'expert', 2, 0, tiled=True)  18.9 us
  transfers between devices with their start and end apart: 8, of which 5 were waited for; matrix products, arithmetic and copies ran while one was open for 35% of the time, Pallas kernels for 0%

commit v1 on v0

v1 whole, which is shorter than its diff:
```python
import jax
import jax.numpy as jnp
from jax import lax
from jax.sharding import PartitionSpec as P

F32 = jnp.float32
BF16 = jnp.bfloat16


def earlier_counts(member):
    tokens = member.shape[-1]
    tok_ids = jnp.arange(tokens, dtype=jnp.int32)
    before = (tok_ids[:, None] < tok_ids[None, :]).astype(BF16)
    return jnp.dot(member.astype(BF16), before, preferred_element_type=F32).astype(jnp.int32)


def solution(mesh):
    stages = mesh.shape["stage"]
    groups = mesh.shape["expert"]
    send_next = [(src, (src + 1) % stages) for src in range(stages)]
    send_back = [(src, (src - 1) % stages) for src in range(stages)]
    tok_spec = P("stage", "expert", None)
    w_spec = P("stage", "expert", None, None)

    def device_step(x_act, route_idx, route_gate, w_up, w_lin, w_down, dy_out):
        tokens = x_act.shape[1]
        local = w_up.shape[1]
        num_experts = local * groups
        capacity = 4 * tokens // num_experts
        slots = jnp.arange(capacity, dtype=jnp.int32)

        meta = jnp.concatenate([route_idx[0].T.astype(F32), route_gate[0].T], axis=0)
        meta = lax.ppermute(meta, "stage", send_next)
        x_tok = lax.ppermute(x_act[0], "stage", send_next)
        meta_all = lax.all_gather(meta, "expert")
        dy_all = lax.all_gather(dy_out[0], "expert")
        x_all = lax.all_gather(x_tok, "expert")

        first = lax.axis_index("expert") * local
        idx_all = meta_all[:, :2].astype(jnp.int32)
        gate_all = meta_all[:, 2:]
        mine = idx_all[:, None] == (first + jnp.arange(local, dtype=jnp.int32))[None, :, None, None]
        member = jnp.any(mine, axis=2)
        gate_m = jnp.sum(jnp.where(mine, gate_all[:, None], 0.0), axis=2)
        pos = earlier_counts(member.reshape(groups * local, tokens)).reshape(groups, local, tokens)
        pos = jnp.where(member, pos, -1)
        hot = pos[:, :, None, :] == slots[None, None, :, None]
        slot_gate = jnp.sum(jnp.where(hot, gate_m[:, :, None, :], 0.0), axis=3)
        hot = hot.astype(BF16)

        idx_own = meta[:2].astype(jnp.int32)
        gate_own = meta[2:]
        is_exp = idx_own[:, None, :] == jnp.arange(num_experts, dtype=jnp.int32)[None, :, None]
        pos_own = earlier_counts(jnp.any(is_exp, axis=0))
        slot_own = jnp.sum(jnp.where(is_exp, pos_own[None], 0), axis=1)
        dev_own = idx_own // local
        loc_own = idx_own % local
        flat = dev_own * capacity + slot_own

        x_rows, d_rows = [], []
        for l in range(local):
            d = jnp.einsum("ist,itd->isd", hot[:, l], dy_all, preferred_element_type=F32)
            d_rows.append((slot_gate[:, l, :, None] * d).astype(BF16).reshape(groups * capacity, -1))
        d_hid = [jnp.dot(d_rows[l], w_down[0, l].T, preferred_element_type=F32).astype(BF16) for l in range(local)]

        dx_back, o_rows, grads = [], [], []
        for l in range(local):
            x = jnp.einsum("ist,itd->isd", hot[:, l], x_all, preferred_element_type=F32).astype(BF16)
            x = x.reshape(groups * capacity, -1)
            a = jnp.dot(x, w_up[0, l], preferred_element_type=F32)
            b = jnp.dot(x, w_lin[0, l], preferred_element_type=F32)
            sig = jax.nn.sigmoid(a)
            act = a * sig
            hid = (act * b).astype(BF16)
            dh = d_hid[l].astype(F32)
            da = (dh * b * sig * (1.0 + a * (1.0 - sig))).astype(BF16)
            db = (dh * act).astype(BF16)
            dx = (jnp.dot(da, w_up[0, l].T, preferred_element_type=F32) + jnp.dot(db, w_lin[0, l].T, preferred_element_type=F32)).astype(BF16)
            dx_back.append(lax.all_to_all(dx.reshape(groups, capacity, -1), "expert", 0, 0, tiled=True))
            o_rows.append(jnp.dot(hid, w_down[0, l], preferred_element_type=F32).astype(BF16))
            grads.append((x, da, db, hid, d_rows[l]))
        o_back = [lax.all_to_all(o_rows[l].reshape(groups, capacity, -1), "expert", 0, 0, tiled=True) for l in range(local)]

        def wgrad(lhs, rhs):
            return jnp.einsum("rd,rf->df", lhs, rhs, preferred_element_type=F32).astype(BF16)

        g_up = jnp.stack([wgrad(g[0], g[1]) for g in grads])
        g_lin = jnp.stack([wgrad(g[0], g[2]) for g in grads])
        g_down = jnp.stack([wgrad(g[3], g[4]) for g in grads])

        cells = jnp.arange(groups * capacity, dtype=jnp.int32)
        dx_sum = jnp.zeros((), F32)
        y_sum = jnp.zeros((), F32)
        for l in range(local):
            at = jnp.where(loc_own == l, flat, -1)
            place = at[:, :, None] == cells[None, None, :]
            both = jnp.any(place, axis=0).astype(BF16)
            dx_sum = dx_sum + jnp.dot(both, dx_back[l].reshape(groups * capacity, -1), preferred_element_type=F32)
        dx_prev = lax.ppermute(dx_sum.astype(BF16), "stage", send_back)
        for l in range(local):
            at = jnp.where(loc_own == l, flat, -1)
            place = (at[:, :, None] == cells[None, None, :]).astype(BF16)
            copies = jnp.einsum("jtc,cd->jtd", place, o_back[l].reshape(groups * capacity, -1), preferred_element_type=F32)
            y_sum = y_sum + jnp.sum(gate_own[:, :, None] * copies, axis=0)
        return y_sum.astype(BF16)[None], dx_prev[None], g_up[None], g_lin[None], g_down[None]

    return jax.shard_map(device_step, mesh=mesh, in_specs=(tok_spec, tok_spec, tok_spec, w_spec, w_spec, w_spec, tok_spec), out_specs=(tok_spec, tok_spec, w_spec, w_spec, w_spec), check_vma=False)
```

time: 567 us -> 517 us (0.912)
  local copies, waits for them, and re-layouts: 82 us -> 6.75 us
  waiting for transfers between devices: 211 us -> 192 us
  between operations: 1.21 us -> 15 us
  matrix products: 220 us -> 233 us
  blocking collectives: 0 us -> 9.63 us
  other arithmetic: 16.4 us -> 25.3 us
    all_to_all x4, waiting for transfers between devices: 175 us -> 79.7 us  [the longest x2 40.5 us: device_step(): lax.all_to_all(o_rows[l].reshape(groups, capacity, -1), 'expert', 0, 0, t...]
    all_gather x0 -> x2, waiting for transfers between devices: none -> 58.3 us  [the longest x1 47.2 us: device_step(): x_all = lax.all_gather(x_tok, 'expert')]
    broadcast_in_dim x2 -> x0, local copies, waits for them, and re-layouts: 45.6 us -> none  [to_owners(): back_rows = lax.all_to_all(expert_rows[None], 'expert', 2, 0, tiled=True)]
    all_to_all x4 -> x0, local copies, waits for them, and re-layouts: 35 us -> none  [the longest x2 18.9 us: to_owners(): back_rows = lax.all_to_all(expert_rows[None], 'expert', 2, 0, tiled=True)]
    dot_general x14 -> x28, matrix products: 220 us -> 233 us  [the longest x6 34.1 us: wgrad(): jnp.einsum('rd,rf->df', lhs, rhs, preferred_element_type=F32).astype(BF16)]
    ppermute x1, waiting for transfers between devices: 36.9 us -> 48.1 us  [device_step(): x_tok = lax.ppermute(x_act[0], 'stage', send_next)]
    reduce_sum x2 -> x3, other arithmetic: 11.8 us -> 2.06 us  [the longest x1 1.94 us: device_step(): slot_gate = jnp.sum(jnp.where(hot, gate_m[:, :, None, :], 0.0), axis=3)]
    all_gather x0 -> x1, blocking collectives: none -> 9.63 us  [device_step(): meta_all = lax.all_gather(meta, 'expert')]
  transfers between devices with their start and end apart: 8 -> 9, of which waited for: 5 -> 9; matrix products, arithmetic and copies ran while one was open for 35% -> 36% of each run, Pallas kernels for 0% -> 0%
where the time goes in v1:
time: 517 us; the launch traced here: 508 us
  matrix products  233 us (45%)
  waiting for transfers between devices  192 us (37%)
  starting transfers between devices  25.8 us (5%)
  other arithmetic  25.3 us (5%)
  between operations  15 us (3%)
  blocking collectives  9.63 us (2%)
  local copies, waits for them, and re-layouts  6.75 us (1%)
    ppermute x1, waiting for transfers between devices, device_step(): x_tok = lax.ppermute(x_act[0], 'stage', send_next)  48.1 us
    all_gather x1, waiting for transfers between devices, device_step(): x_all = lax.all_gather(x_tok, 'expert')  47.2 us
    all_to_all x2, waiting for transfers between devices, device_step(): lax.all_to_all(o_rows[l].reshape(groups, capacity, -1), 'expert', 0, 0, t...  40.5 us
    all_to_all x2, waiting for transfers between devices, device_step(): lax.all_to_all(dx.reshape(groups, capacity, -1), 'expert', 0, 0, tiled=True)  39.2 us
    dot_general x6, matrix products, wgrad(): jnp.einsum('rd,rf->df', lhs, rhs, preferred_element_type=F32).astype(BF16)  34.1 us
    dot_general x2, matrix products, device_step(): b = jnp.dot(x, w_lin[0, l], preferred_element_type=F32)  28.6 us
    dot_general x2, matrix products, device_step(): jnp.einsum('jtc,cd->jtd', place, o_back[l].reshape(groups * capacity, -1)...  26.7 us
    dot_general x2, matrix products, device_step(): jnp.einsum('ist,itd->isd', hot[:, l], dy_all, preferred_element_type=F32)  25.9 us
  transfers between devices with their start and end apart: 9, of which 9 were waited for; matrix products, arithmetic and copies ran while one was open for 36% of the time, Pallas kernels for 0%

profile of v1, /device:TPU:0, one launch (start us, length us, event | category | flops | bytes accessed | tf_op | source)
XLA Modules:
  0.0 507.9 jit_solution(6375934935475491766)
XLA Ops:
  11.1 48.1 %collective-permute-done.1 = bf16[1024,1024]{1,0:T(8,128)(2,1)S(1)} collective-permute-done((bf16[1024,1024]{1,0:T(8,128)(2,1)}, bf16[1024,1024]{1,0:T(8,128)(2,1)S(1)}, u32[]{:S(2)}, u32[]{:S(2)}) %collective-permute-start.1) | collective-permute-done | bytes 2097184 | tf_op jit(solution)/shard_map/ppermute | solution.py:34
  66.2 9.6 %all-gather.2 = f32[8,4,1024]{2,1,0:T(4,128)S(1)} all-gather(f32[1,4,1024]{2,1,0:T(4,128)S(1)} %bitcast.142), channel_id=2, replica_groups=mesh['stage'=4,'expert'=8] {'expert'}, dimensions={0}, use_global_device_ids=true | all-gather | bytes 147456 | tf_op jit(solution)/shard_map/all_gather | solution.py:35
  91.9 11.0 %all-gather.6.cloned.1.call-done = bf16[8,1024,1024]{2,1,0:T(8,128)(2,1)} async-done(((bf16[1,1024,1024]{2,1,0:T(8,128)(2,1)}), bf16[8,1024,1024]{2,1,0:T(8,128)(2,1)}) %all-gather.6.cloned.1.call-update) | async-done | bytes 16777232 | tf_op jit(solution)/shard_map/all_gather | solution.py:36
  102.9 13.2 %multiply_convert_fusion.1 = bf16[8,256,1024]{2,1,0:T(8,128)(2,1)} fusion(f32[8,256]{1,0:T(8,128)S(1)} %get-tuple-element.17, bf16[8,1024,1024]{2,1,0:T(8,128)(2,1)} %all-gather.6.cloned.1.call-done, pred[8,2,256,1024]{3,2,0,1:T(32,128)(4,1)} %iota_compare_fusion.2), kind=kOutput, calls=%fused_computation.23 | convolution fusion | flops 4299161600 | bytes 23076864 | tf_op jit(solution)/shard_map/ist,itd->isd/dot_general | solution.py:62
  116.1 9.6 %convolution_convert_fusion.1 = bf16[2048,1024]{1,0:T(8,128)(2,1)} fusion(bf16[2048,1024]{1,0:T(8,128)(2,1)} %bitcast.151, bf16[1,2,1024,1024]{3,2,1,0:T(8,128)(2,1)} %param.12), kind=kOutput, calls=%fused_computation.49 | convolution fusion | flops 4297064448 | bytes 10485760 | tf_op jit(solution)/shard_map/dot_general | solution.py:64
  125.7 12.7 %multiply_convert_fusion = bf16[8,256,1024]{2,1,0:T(8,128)(2,1)} fusion(f32[8,256]{1,0:T(8,128)S(1)} %get-tuple-element.16, bf16[8,1024,1024]{2,1,0:T(8,128)(2,1)} %all-gather.6.cloned.1.call-done, pred[8,2,256,1024]{3,2,0,1:T(32,128)(4,1)S(1)} %copy-done), kind=kOutput, calls=%fused_computation.21 | convolution fusion | flops 4299161600 | bytes 23076864 | tf_op jit(solution)/shard_map/ist,itd->isd/dot_general | solution.py:62
  138.4 9.4 %convolution_convert_fusion = bf16[2048,1024]{1,0:T(8,128)(2,1)} fusion(bf16[2048,1024]{1,0:T(8,128)(2,1)} %bitcast.157, bf16[1,2,1024,1024]{3,2,1,0:T(8,128)(2,1)} %param.12), kind=kOutput, calls=%fused_computation.48 | convolution fusion | flops 4297064448 | bytes 10485760 | tf_op jit(solution)/shard_map/dot_general | solution.py:64
  147.8 47.2 %all-gather.8.cloned.1.call-done = bf16[8192,1024]{1,0:T(8,128)(2,1)} async-done(((bf16[1024,1024]{1,0:T(8,128)(2,1)}), bf16[8192,1024]{1,0:T(8,128)(2,1)}) %all-gather.8.cloned.1.call-update) | async-done | bytes 16777232 | tf_op jit(solution)/shard_map/all_gather | solution.py:37
  195.0 13.1 %fusion.22 = bf16[8,256,1024]{2,1,0:T(8,128)(2,1)} fusion(bf16[8,1024,1024]{2,1,0:T(8,128)(2,1)} %bitcast.144, pred[8,2,256,1024]{3,2,0,1:T(32,128)(4,1)} %iota_compare_fusion.2), kind=kOutput, calls=%fused_computation.52 | convolution fusion | flops 4297064448 | bytes 23068672 | tf_op jit(solution)/shard_map/ist,itd->isd/dot_general | solution.py:68
  208.1 12.6 %fusion.23 = bf16[8,256,1024]{2,1,0:T(8,128)(2,1)} fusion(bf16[8,1024,1024]{2,1,0:T(8,128)(2,1)} %bitcast.145, pred[8,2,256,1024]{3,2,0,1:T(32,128)(4,1)S(1)} %copy-done.1), kind=kOutput, calls=%fused_computation.53 | convolution fusion | flops 4297064448 | bytes 23068672 | tf_op jit(solution)/shard_map/ist,itd->isd/dot_general | solution.py:68
  220.7 9.2 %fusion.32 = f32[2048,1024]{1,0:T(8,128)} fusion(bf16[2048,1024]{1,0:T(8,128)(2,1)} %bitcast.153, bf16[1,2,1024,1024]{3,2,1,0:T(8,128)(2,1)S(1)} %copy-done.15), kind=kOutput, calls=%fused_computation.62 | convolution fusion | flops 4294967296 | bytes 14680064 | tf_op jit(solution)/shard_map/dot_general | solution.py:70
  229.9 14.4 %fusion.10 = (bf16[2048,1024]{1,0:T(8,128)(2,1)}, bf16[2048,1024]{1,0:T(8,128)(2,1)}, bf16[2048,1024]{1,0:T(8,128)(2,1)}) fusion(bf16[2048,1024]{1,0:T(8,128)(2,1)} %convolution_convert_fusion, f32[2048,1024]{1,0:T(8,128)} %fusion.32, bf16[2048,1024]{1,0:T(8,128)(2,1)S(1)} %bitcast.154, bf16[1,2,1024,1024]{3,2,1,0:T(8,128)(2,1)S(1)} %copy-done.17), kind=kOutput, calls=%fused_computation.18 | convolution fusion | flops 4328521728 | bytes 31457280 | tf_op jit(solution)/shard_map/dot_general | solution.py:71
  244.3 7.1 %convert_bitcast_fusion = bf16[1,1024,1024]{2,1,0:T(8,128)(2,1)S(1)} fusion(bf16[2048,1024]{1,0:T(8,128)(2,1)} %get-tuple-element.9, bf16[2048,1024]{1,0:T(8,128)(2,1)S(1)} %bitcast.158), kind=kOutput, calls=%fused_computation.73 | convolution fusion | flops 4296015872 | bytes 10485760 | tf_op jit(solution)/shard_map/rd,rf->df/dot_general | solution.py:85
  262.8 6.6 %add_convert_fusion = bf16[2048,1024]{1,0:T(8,128)(2,1)} fusion(f32[2048,1024]{1,0:T(8,128)S(1)} %fusion.30, bf16[2048,1024]{1,0:T(8,128)(2,1)S(1)} %copy-done.33, bf16[1,2,1024,1024]{3,2,1,0:T(8,128)(2,1)S(1)} %copy-done.17), kind=kOutput, calls=%fused_computation.20 | convolution fusion | flops 4299161600 | bytes 18874368 | tf_op jit(solution)/shard_map/dot_general | solution.py:78
  274.5 10.8 %fusion.41 = f32[2048,1024]{1,0:T(8,128)} fusion(bf16[2048,1024]{1,0:T(8,128)(2,1)} %bitcast.147, bf16[1,2,1024,1024]{3,2,1,0:T(8,128)(2,1)} %param.10), kind=kOutput, calls=%fused_computation.71 | convolution fusion | flops 4294967296 | bytes 14680064 | tf_op jit(solution)/shard_map/dot_general | solution.py:70
  291.1 14.2 %fusion.6 = (bf16[2048,1024]{1,0:T(8,128)(2,1)}, bf16[2048,1024]{1,0:T(8,128)(2,1)}, bf16[2048,1024]{1,0:T(8,128)(2,1)}) fusion(bf16[2048,1024]{1,0:T(8,128)(2,1)} %convolution_convert_fusion.1, f32[2048,1024]{1,0:T(8,128)} %fusion.41, bf16[2048,1024]{1,0:T(8,128)(2,1)S(1)} %bitcast.148, bf16[1,2,1024,1024]{3,2,1,0:T(8,128)(2,1)S(1)} %copy-done.18), kind=kOutput, calls=%fused_computation.14 | convolution fusion | flops 4328521728 | bytes 31457280 | tf_op jit(solution)/shard_map/dot_general | solution.py:71
  305.3 18.2 %all-to-all-done.3 = bf16[8,256,1024]{2,1,0:T(8,128)(2,1)} async-done(((bf16[8,256,1024]{2,1,0:T(8,128)(2,1)}), bf16[8,256,1024]{2,1,0:T(8,128)(2,1)}, u32[]{:S(2)}, u32[]{:S(2)}) %all-to-all-start.3) | async-done | bytes 4194336 | tf_op jit(solution)/shard_map/all_to_all | solution.py:79
  328.2 7.1 %fusion.39 = f32[2048,1024]{1,0:T(8,128)S(1)} fusion(bf16[2048,1024]{1,0:T(8,128)(2,1)} %get-tuple-element.10, bf16[1,2,1024,1024]{3,2,1,0:T(8,128)(2,1)} %param.10), kind=kOutput, calls=%fused_computation.69 | convolution fusion | flops 4294967296 | bytes 14680064 | tf_op jit(solution)/shard_map/dot_general | solution.py:78
  353.7 23.5 %all-to-all-done.1 = bf16[8,256,1024]{2,1,0:T(8,128)(2,1)} async-done(((bf16[8,256,1024]{2,1,0:T(8,128)(2,1)}), bf16[8,256,1024]{2,1,0:T(8,128)(2,1)}, u32[]{:S(2)}, u32[]{:S(2)}) %all-to-all-start.1) | async-done | bytes 4194336 | tf_op jit(solution)/shard_map/all_to_all | solution.py:82
  410.0 21.0 %all-to-all-done.2 = bf16[8,256,1024]{2,1,0:T(8,128)(2,1)} async-done(((bf16[8,256,1024]{2,1,0:T(8,128)(2,1)}), bf16[8,256,1024]{2,1,0:T(8,128)(2,1)}, u32[]{:S(2)}, u32[]{:S(2)}) %all-to-all-start.2) | async-done | bytes 4194336 | tf_op jit(solution)/shard_map/all_to_all | solution.py:79
  442.2 7.9 %add_convert_fusion.2 = bf16[1024,1024]{1,0:T(8,128)(2,1)} fusion(f32[1024,1024]{1,0:T(8,128)S(1)} %fusion.60, pred[1024,2048]{1,0:T(8,128)(4,1)S(1)} %copy-done.3, bf16[2048,1024]{1,0:T(8,128)(2,1)} %bitcast.31), kind=kOutput, calls=%fused_computation.43 | convolution fusion | flops 4297064448 | bytes 12582912 | tf_op jit(solution)/shard_map/dot_general | solution.py:98
  453.5 14.3 %multiply_reduce_fusion = f32[1024,1024]{1,0:T(8,128)} fusion(f32[2,1024]{1,0:T(2,128)S(1)} %copy-done.14, bf16[2048,1024,1]{1,0,2:T(8,128)(2,1)} %bitcast.22, s32[2,1024]{1,0:T(2,128)S(1)} %copy-done.11), kind=kOutput, calls=%fused_computation.24 | convolution fusion | flops 8597274624 | bytes 8404992 | tf_op jit(solution)/shard_map/jtc,cd->jtd/dot_general | solution.py:103
  467.7 17.0 %all-to-all-done = bf16[8,256,1024]{2,1,0:T(8,128)(2,1)} async-done(((bf16[8,256,1024]{2,1,0:T(8,128)(2,1)}), bf16[8,256,1024]{2,1,0:T(8,128)(2,1)}, u32[]{:S(2)}, u32[]{:S(2)}) %all-to-all-start) | async-done | bytes 4194336 | tf_op jit(solution)/shard_map/all_to_all | solution.py:82
  484.7 12.4 %multiply_reduce_fusion.1 = f32[1024,1024]{1,0:T(8,128)S(1)} fusion(f32[2,1024]{1,0:T(2,128)S(1)} %copy-done.14, bf16[2048,1024,1]{1,0,2:T(8,128)(2,1)} %bitcast.14, s32[2,1024]{1,0:T(2,128)S(1)} %copy-done.9), kind=kOutput, calls=%fused_computation.29 | convolution fusion | flops 8597274624 | bytes 8404992 | tf_op jit(solution)/shard_map/jtc,cd->jtd/dot_general | solution.py:103
  (129 shorter events, 122.5 us)
Async XLA Ops:
  7.2 53.4 %copy-start.12 = (s32[1,1024,2]{1,2,0:T(2,128)S(1)}, s32[1,1024,2]{1,2,0:T(2,128)}, u32[]{:S(2)}) copy-start(s32[1,1024,2]{1,2,0:T(2,128)} %param.8) | copy-start | bytes 24580
  7.2 53.4 %copy-start.13 = (f32[1,1024,2]{1,2,0:T(2,128)S(1)}, f32[1,1024,2]{1,2,0:T(2,128)}, u32[]{:S(2)}) copy-start(f32[1,1024,2]{1,2,0:T(2,128)} %param.9) | copy-start | bytes 24580
  7.2 95.7 %all-gather.6.cloned.1.call-start = ((), (), s32[]{:S(2)}) async-start(), calls=%async_computation.4 | async-start | bytes 18874368 | tf_op jit(solution)/shard_map/all_gather | solution.py:36
  7.9 187.1 %all-gather.8.cloned.1.call-start = ((), (), s32[]{:S(2)}) async-start(), calls=%async_computation.5 | async-start | bytes 18874368 | tf_op jit(solution)/shard_map/all_gather | solution.py:37
  8.0 51.3 %collective-permute-start.1 = (bf16[1024,1024]{1,0:T(8,128)(2,1)}, bf16[1024,1024]{1,0:T(8,128)(2,1)S(1)}, u32[]{:S(2)}, u32[]{:S(2)}) collective-permute-start(bf16[1024,1024]{1,0:T(8,128)(2,1)} %bitcast.146), channel_id=1, source_target_pairs={{0,8},{8,16},{16,24},{24,0},{1,9},{9,17},{17,25},{25,1},{2,10},{10... | collective-permute-start | bytes 6291464 | tf_op jit(solution)/shard_map/ppermute | solution.py:34
  60.6 5.6 %collective-permute-start = (f32[4,1024]{1,0:T(4,128)S(1)}, f32[4,1024]{1,0:T(4,128)S(1)}, u32[]{:S(2)}, u32[]{:S(2)}) collective-permute-start(f32[4,1024]{1,0:T(4,128)S(1)} %pad_maximum_fusion), channel_id=1, source_target_pairs={{0,8},{8,16},{16,24},{24,0},{1,9},{9,17},{17,25},{25,1},{2,10},{10... | collective-permute-start | bytes 49160 | tf_op jit(solution)/shard_map/ppermute | solution.py:33
  116.1 9.6 %copy-start = (pred[8,2,256,1024]{3,2,0,1:T(32,128)(4,1)S(1)}, pred[8,2,256,1024]{3,2,0,1:T(32,128)(4,1)}, u32[]{:S(2)}) copy-start(pred[8,2,256,1024]{3,2,0,1:T(32,128)(4,1)} %iota_compare_fusion.2) | copy-start | bytes 12582916
  195.0 13.1 %copy-start.1 = (pred[8,2,256,1024]{3,2,0,1:T(32,128)(4,1)S(1)}, pred[8,2,256,1024]{3,2,0,1:T(32,128)(4,1)}, u32[]{:S(2)}) copy-start(pred[8,2,256,1024]{3,2,0,1:T(32,128)(4,1)} %iota_compare_fusion.2) | copy-start | bytes 12582916
  208.1 12.6 %copy-start.15 = (bf16[1,2,1024,1024]{3,2,1,0:T(8,128)(2,1)S(1)}, bf16[1,2,1024,1024]{3,2,1,0:T(8,128)(2,1)}, u32[]{:S(2)}) copy-start(bf16[1,2,1024,1024]{3,2,1,0:T(8,128)(2,1)} %param.10) | copy-start | bytes 12582916
  220.7 9.2 %copy-start.17 = (bf16[1,2,1024,1024]{3,2,1,0:T(8,128)(2,1)S(1)}, bf16[1,2,1024,1024]{3,2,1,0:T(8,128)(2,1)}, u32[]{:S(2)}) copy-start(bf16[1,2,1024,1024]{3,2,1,0:T(8,128)(2,1)} %param.11) | copy-start | bytes 12582916
  220.7 9.2 %copy-start.25 = (bf16[8,256,1024]{2,1,0:T(8,128)(2,1)S(1)}, bf16[8,256,1024]{2,1,0:T(8,128)(2,1)}, u32[]{:S(2)}) copy-start(bf16[8,256,1024]{2,1,0:T(8,128)(2,1)} %fusion.22) | copy-start | bytes 12582916
  229.9 14.4 %copy-start.28 = (bf16[8,256,1024]{2,1,0:T(8,128)(2,1)S(1)}, bf16[8,256,1024]{2,1,0:T(8,128)(2,1)}, u32[]{:S(2)}) copy-start(bf16[8,256,1024]{2,1,0:T(8,128)(2,1)} %multiply_convert_fusion) | copy-start | bytes 12582916
  269.4 54.0 %all-to-all-start.3 = ((bf16[8,256,1024]{2,1,0:T(8,128)(2,1)}), bf16[8,256,1024]{2,1,0:T(8,128)(2,1)}, u32[]{:S(2)}, u32[]{:S(2)}) async-start(bf16[8,256,1024]{2,1,0:T(8,128)(2,1)} %bitcast.140), calls=%async_computation.3 | async-start | bytes 8388608 | tf_op jit(solution)/shard_map/all_to_all | solution.py:79
  274.4 10.8 %copy-start.26 = (bf16[8,256,1024]{2,1,0:T(8,128)(2,1)S(1)}, bf16[8,256,1024]{2,1,0:T(8,128)(2,1)}, u32[]{:S(2)}) copy-start(bf16[8,256,1024]{2,1,0:T(8,128)(2,1)} %fusion.22) | copy-start | bytes 12582916
  274.5 10.8 %copy-start.37 = (bf16[2048,1024]{1,0:T(8,128)(2,1)S(1)}, bf16[2048,1024]{1,0:T(8,128)(2,1)}, u32[]{:S(2)}) copy-start(bf16[2048,1024]{1,0:T(8,128)(2,1)} %get-tuple-element.8) | copy-start | bytes 12582916
  323.5 53.8 %all-to-all-start.1 = ((bf16[8,256,1024]{2,1,0:T(8,128)(2,1)}), bf16[8,256,1024]{2,1,0:T(8,128)(2,1)}, u32[]{:S(2)}, u32[]{:S(2)}) async-start(bf16[8,256,1024]{2,1,0:T(8,128)(2,1)} %bitcast.137), calls=%async_computation.1 | async-start | bytes 8388608 | tf_op jit(solution)/shard_map/all_to_all | solution.py:82
  328.2 7.2 %copy-start.27 = (bf16[8,256,1024]{2,1,0:T(8,128)(2,1)S(1)}, bf16[8,256,1024]{2,1,0:T(8,128)(2,1)}, u32[]{:S(2)}) copy-start(bf16[8,256,1024]{2,1,0:T(8,128)(2,1)} %fusion.22) | copy-start | bytes 12582916
  377.2 53.8 %all-to-all-start.2 = ((bf16[8,256,1024]{2,1,0:T(8,128)(2,1)}), bf16[8,256,1024]{2,1,0:T(8,128)(2,1)}, u32[]{:S(2)}, u32[]{:S(2)}) async-start(bf16[8,256,1024]{2,1,0:T(8,128)(2,1)} %bitcast.138), calls=%async_computation.2 | async-start | bytes 8388608 | tf_op jit(solution)/shard_map/all_to_all | solution.py:79
  431.0 53.7 %all-to-all-start = ((bf16[8,256,1024]{2,1,0:T(8,128)(2,1)}), bf16[8,256,1024]{2,1,0:T(8,128)(2,1)}, u32[]{:S(2)}, u32[]{:S(2)}) async-start(bf16[8,256,1024]{2,1,0:T(8,128)(2,1)} %bitcast.139), calls=%async_computation | async-start | bytes 8388608 | tf_op jit(solution)/shard_map/all_to_all | solution.py:82
  442.2 11.3 %copy-start.11 = (s32[2,1024]{1,0:T(2,128)S(1)}, s32[2,1024]{1,0:T(2,128)}, u32[]{:S(2)}) copy-start(s32[2,1024]{1,0:T(2,128)} %copy-done.10) | copy-start | bytes 24580
  442.2 11.3 %copy-start.14 = (f32[2,1024]{1,0:T(2,128)S(1)}, f32[2,1024]{1,0:T(2,128)}, u32[]{:S(2)}) copy-start(f32[2,1024]{1,0:T(2,128)} %get-tuple-element.19) | copy-start | bytes 24580
  450.1 49.2 %collective-permute-start.2 = (bf16[1024,1024]{1,0:T(8,128)(2,1)}, bf16[1024,1024]{1,0:T(8,128)(2,1)S(1)}, u32[]{:S(2)}, u32[]{:S(2)}) collective-permute-start(bf16[1024,1024]{1,0:T(8,128)(2,1)} %add_convert_fusion.2), channel_id=1, source_target_pairs={{0,24},{8,0},{16,8},{24,16},{1,25},{9,1},{17,9},{25,17},{2,26},{10... | collective-permute-start | bytes 6291464 | tf_op jit(solution)/shard_map/ppermute | solution.py:99
  453.5 31.2 %copy-start.9 = (s32[2,1024]{1,0:T(2,128)S(1)}, s32[2,1024]{1,0:T(2,128)}, u32[]{:S(2)}) copy-start(s32[2,1024]{1,0:T(2,128)} %copy-done.8) | copy-start | bytes 24580
  484.7 12.4 %copy-start.2 = (f32[1024,1024]{1,0:T(8,128)S(1)}, f32[1024,1024]{1,0:T(8,128)}, u32[]{:S(2)}) copy-start(f32[1024,1024]{1,0:T(8,128)} %multiply_reduce_fusion) | copy-start | bytes 12582916
  (24 other events, 126.8 us)
Sparse Core Ops, SparseCore 0:
  9.9 92.9 all-gather.5
  105.3 89.6 all-gather.7
